TPU v7x, 512 devices: a whole 4x8x8 slice. The times are simulated.
512 devices in a mesh: box: 128 (over y, z, core), nbr: 4 (over x).
Axes of the slice: x: 4, y: 8, z: 8, core: 2. Of those that a mesh axis runs over, the one named last changes fastest.
Arguments:
- self_block: float32 [1024, 256, 256], P('box', 'nbr'), as said below
- ordering: int32 [1024, 256], P('box'), may hold values from 0 to 255, each once within a row
- interp: float32 [1024, 64, 192], P('box'), may hold values from -0.12 to 0.12
- near_band: float32 [1024, 8, 2, 64, 256], P('box', 'nbr'), may hold values from -3 to 3
- pair_mask: int32 [1024, 8], P('box', 'nbr'), may hold values 0 or 1
Outputs:
- skeleton_self: float32 [1024, 64, 64], P('box')
- red_inverse: float32 [1024, 192, 192], P('box', 'nbr')
- couplings: float32 [1024, 8, 64, 128], P('box', 'nbr')
Inputs may be any that keep to these rules, and one draw needn't show every extreme that they name: Each row of ordering is a permutation of the 256 unknowns of its box. Each self_block[b] has a positive diagonal.
All inputs are finite; a program needn't handle non-finite values. No bound on the sum of `pair_mask` on one device may be relied on, other than what follows from the above.
Results may differ from a plain program's by a relative error of at most 0.0003.
Values sent between devices are 32-bit elements; how exact they have to be, the bound alone decides.
No kernel may reach another device: no remote copies, remote signals or barrier semaphores. Data moves between devices by JAX's collectives and lax.ppermute only.
A program may use at most 128 MiB of HBM per device.

v0:
```python
import jax
import jax.numpy as jnp
from jax import lax
from jax.experimental import pallas as pl
from jax.experimental.pallas import tpu as pltpu
from jax.sharding import PartitionSpec as P

SKEL = 64
RED = 192
PTS = 256
REACH = 4
HALF = 4
PAIR = 128
ROWS = 48
BF = jnp.bfloat16
F32 = jnp.float32
LIMIT = 28 * 1024 * 1024


def split(x):
    high = x.astype(BF)
    return high, (x - high.astype(F32)).astype(BF)


def dot(a, b):
    return jnp.dot(a, b, preferred_element_type=F32)


def dot3(a, b):
    return dot(a[0], b[0]) + dot(a[1], b[0]) + dot(a[0], b[1])


def eye(rows, columns):
    i = lax.broadcasted_iota(jnp.int32, (rows, columns), 0)
    j = lax.broadcasted_iota(jnp.int32, (rows, columns), 1)
    return (i == j).astype(F32)


def slot_offset(place, slot):
    j = place * 2 + slot
    return jnp.where(j < REACH, j - REACH, j - REACH + 1)


def half_of(place, chunk):
    return jnp.where(place < 2, 1 - chunk, chunk)


def choose(boxes, order_ref, interp, mixer, z_ref, zt_ref):
    unknown = lax.broadcasted_iota(jnp.int32, (PTS, PTS), 0)
    upper = eye(RED, PTS).astype(BF)
    nothing = jnp.zeros((RED, PTS), BF)
    for k, box in enumerate(boxes):
        low = jnp.concatenate([-interp[k], eye(SKEL, SKEL)], axis=1)
        mixer[k, 0, :RED], mixer[k, 1, :RED] = upper, nothing
        mixer[k, 0, RED:], mixer[k, 1, RED:] = split(low)
    for k, box in enumerate(boxes):
        order = pltpu.roll(order_ref[pl.ds(box, 1), :], RED, 1)
        chooser = (unknown == order).astype(F32).astype(BF)
        for level in range(2):
            z = dot(chooser, mixer[k, level])
            z_ref[k, level] = z.astype(BF)
            zt_ref[k, level] = z.T.astype(BF)


def source_of(box, place, slot):
    source = box - slot_offset(place, slot)
    inside = jnp.logical_and(source >= 0, source < 2 * HALF)
    return source, inside, jnp.clip(source, 0, 2 * HALF - 1)


def fetch(boxes, place, near_ref, halo_ref, rows_ref, sem):
    waits = []
    for k, box in enumerate(boxes):
        for slot in range(2):
            source, inside, local = source_of(box, place, slot)
            to = rows_ref.at[k, slot]
            flag = sem.at[2 * k + slot]
            near = pltpu.make_async_copy(near_ref.at[local, slot], to, flag)
            waits.append(near)
            if halo_ref is None:
                near.start()
            else:
                remote = jnp.where(source >= 2 * HALF, source - 2 * HALF, source + HALF)
                remote = jnp.clip(remote, 0, HALF - 1)
                far = pltpu.make_async_copy(halo_ref.at[remote, slot], to, flag)
                pl.when(inside)(near.start)
                pl.when(jnp.logical_not(inside))(far.start)
    return waits


def meet(boxes, place, mask_ref, rows_ref, z_ref):
    g, nt = [], []
    for k, box in enumerate(boxes):
        rows = []
        for slot in range(2):
            _, inside, local = source_of(box, place, slot)
            weight = jnp.where(inside, mask_ref[local, slot], 1).astype(F32)
            rows.append(rows_ref[k, slot] * weight)
        stacked = jnp.concatenate([rows[0][0], rows[1][0], rows[0][1], rows[1][1]], axis=0)
        done = dot3(split(stacked), (z_ref[k, 0], z_ref[k, 1]))
        g.append(done[:PAIR])
        nt.append(done[PAIR:].T)
    return g, nt


def factor(place, blocks_ref, z_ref, zt_ref, even, odd, tail, inverse_ref):
    each = range(HALF)
    diagonal = eye(PTS, PTS)
    red_diag = diagonal[:RED]
    column = lax.broadcasted_iota(jnp.int32, (1, PTS), 1)
    moved, diag_row, block, inv = [], [], [], []
    for k in each:
        full = blocks_ref[:, k].reshape(PTS, PTS)
        diag_row.append(jnp.sum(full * diagonal, axis=0, keepdims=True))
        moved.append(split(dot3(split(full), (z_ref[k, 0], z_ref[k, 1]))))
    for k in each:
        block.append(dot3((zt_ref[k, 0], zt_ref[k, 1]), moved[k]))
    for k in each:
        chosen = zt_ref[k, 0].astype(F32)
        order_col = jnp.sum(jnp.where(chosen == 1.0, diag_row[k], 0.0), axis=1, keepdims=True)
        scale = jnp.sum(diagonal * order_col, axis=0, keepdims=True)
        inv.append(jnp.where(column < RED, 1.0 / jnp.where(column < RED, scale, 1.0), 0.0))
    nothing = jnp.zeros((SKEL, PTS), BF)
    e1, e1s, e2, s4 = [], [], [], []
    for k in each:
        for ref in (even, odd):
            ref[k, 0, RED:], ref[k, 1, RED:] = nothing, nothing
        e1.append(jnp.where(column < RED, red_diag - block[k][:RED] * inv[k], 0.0))
        e1s.append(split(e1[k]))
        even[k, 0, :RED], even[k, 1, :RED] = e1s[k]
    for k in each:
        e2.append(dot3(e1s[k], (even[k, 0], even[k, 1])))
        odd[k, 0, :RED], odd[k, 1, :RED] = split(e2[k])
    for k in each:
        e2s = (odd[k, 0, :RED], odd[k, 1, :RED])
        e4 = dot3(e2s, (odd[k, 0], odd[k, 1]))
        s4.append(red_diag + e1[k] + e2[k] + dot3(e1s[k], (odd[k, 0], odd[k, 1])))
        even[k, 0, :RED], even[k, 1, :RED] = split(e4)
    for k in each:
        s8 = s4[k] + dot3(split(s4[k]), (even[k, 0], even[k, 1]))
        odd[k, 0, :RED], odd[k, 1, :RED] = split(s8)
        tail[k] = s8
    i = lax.broadcasted_iota(jnp.int32, (ROWS, PTS), 0) + place * ROWS
    j = lax.broadcasted_iota(jnp.int32, (ROWS, PTS), 1)
    start = pl.multiple_of(place * ROWS, 8)
    for k in each:
        inv_col = jnp.sum(jnp.where(i == j, inv[k], 0.0), axis=1, keepdims=True)
        inverse_ref[k] = (tail[k, pl.ds(start, ROWS), :] * inv_col)[:, :RED]
    skel = [block[k][RED:] for k in each]
    side = [block[k][:, PAIR:] for k in each]
    return inv, skel, side


def finish(boxes, place, inv, skel, side, g, nt, s_ref, couple_ref, own_ref, extended):
    each = range(HALF)
    lane = lax.broadcasted_iota(jnp.int32, (SKEL, PAIR), 1)
    left = lane < SKEL
    carried, last = [], []
    for k in each:
        mine = jnp.concatenate([skel[k], g[k]], axis=0) * inv[k]
        carried.append(dot3(split(mine), (s_ref[k, 0], s_ref[k, 1])))
    for k in each:
        right = split(jnp.concatenate([nt[k], side[k]], axis=1))
        last.append(dot3(split(carried[k]), right))
    for k in each:
        end = last[k]
        own_ref[k] = (skel[k][:, PAIR:] - end[:SKEL, PAIR:])[:, SKEL:]
        forward = nt[k][RED:] - end[:SKEL, :PAIR]
        backward = (g[k][:, PAIR:] - end[SKEL:, PAIR:]).T[SKEL:]
        couple_ref[k, 0] = jnp.where(left, forward, pltpu.roll(backward, SKEL, 1))
        couple_ref[k, 1] = jnp.where(left, pltpu.roll(forward, SKEL, 1), backward)
    for k, box in enumerate(boxes):
        first = box - slot_offset(place, 0) + REACH
        second = box - slot_offset(place, 1) + REACH
        extended[first] += jnp.where(left, last[k][SKEL:PAIR, :PAIR], 0.0)
        extended[second] += jnp.where(left, 0.0, last[k][PAIR:, :PAIR])
    return left


def doubled(x):
    return x + pltpu.roll(x, SKEL, 1)


def packed(extended, left):
    return [
        jnp.where(left, doubled(extended[REACH + k]), doubled(extended[REACH + HALF + k]))
        for k in range(HALF)
    ]


def boxes_of(place, chunk):
    base = half_of(place, chunk) * HALF
    return [base + k for k in range(HALF)]


def started(copies):
    for copy in copies:
        copy.start()
    return copies


def ended(copies):
    for copy in copies:
        copy.wait()


def half_rows(ref, place, chunk):
    return ref.at[pl.ds(half_of(place, chunk) * HALF, HALF)]


def factor_kernel(
    place_ref, order_ref, interp_ref, first_ref,
    inverse_ref, z_ref, s_ref, inv_ref, skel_ref, side_ref,
    blocks_ref, interp, zt_ref, even, tail, sem,
):
    place = place_ref[0]
    needs = started([
        pltpu.make_async_copy(half_rows(interp_ref, place, 0), interp, sem.at[0]),
        pltpu.make_async_copy(first_ref, blocks_ref, sem.at[1]),
    ])
    ended(needs[:1])
    choose(boxes_of(place, 0), order_ref, interp, even, z_ref, zt_ref)
    ended(needs[1:])
    inv, skel, side = factor(place, blocks_ref, z_ref, zt_ref, even, s_ref, tail, inverse_ref)
    for k in range(HALF):
        inv_ref[k] = jnp.broadcast_to(inv[k], (8, PTS))
        skel_ref[k], side_ref[k] = skel[k], side[k]


def edge_kernel(
    place_ref, mask_ref, near_ref, halo_ref, z_ref, s_ref, inv_ref, skel_ref, side_ref,
    couple_ref, own_ref, kept_ref, leaving_ref, rows_ref, extended, sem,
):
    place = place_ref[0]
    boxes = boxes_of(place, 0)
    waits = fetch(boxes, place, near_ref, halo_ref, rows_ref, sem)
    extended[...] = jnp.zeros_like(extended)
    ended(waits)
    g, nt = meet(boxes, place, mask_ref, rows_ref, z_ref)
    inv = [inv_ref[k, :1] for k in range(HALF)]
    skel = [skel_ref[k] for k in range(HALF)]
    side = [side_ref[k] for k in range(HALF)]
    left = finish(boxes, place, inv, skel, side, g, nt, s_ref, couple_ref, own_ref, extended)
    for k, value in enumerate(packed(extended, left)):
        kept_ref[k] = value
    beyond = jnp.where(place < 2, REACH + 2 * HALF, 0)
    for k in range(HALF):
        leaving_ref[k] = doubled(extended[beyond + k])


def inner_kernel(
    place_ref, mask_ref, order_ref, interp_ref, near_ref, block_ref, came_1, came_2, came_3,
    kept_in, inverse_in, couple_in, own_in,
    inverse_ref, couple_ref, own_ref, total_ref,
    blocks_ref, interp, rows_ref, z_ref, zt_ref, even, odd, tail, extended, sem,
):
    place = place_ref[0]
    boxes = boxes_of(place, 1)
    text = started([pltpu.make_async_copy(half_rows(interp_ref, place, 1), interp, sem.at[8])])
    parts = started([
        pltpu.make_async_copy(source, blocks_ref.at[lax.rem(place + 4 - k, 4)], sem.at[9 + k])
        for k, source in enumerate([half_rows(block_ref, place, 1), came_1, came_2, came_3])
    ])
    waits = fetch(boxes, place, near_ref, None, rows_ref, sem)
    extended[...] = jnp.zeros_like(extended)
    ended(text)
    choose(boxes, order_ref, interp, even, z_ref, zt_ref)
    ended(parts)
    inv, skel, side = factor(place, blocks_ref, z_ref, zt_ref, even, odd, tail, inverse_ref)
    ended(waits)
    g, nt = meet(boxes, place, mask_ref, rows_ref, z_ref)
    left = finish(boxes, place, inv, skel, side, g, nt, odd, couple_ref, own_ref, extended)
    for k, value in enumerate(packed(extended, left)):
        total_ref[k] = value + kept_in[k]


def call(kernel, place, args, outs, scratch, aliases=None):
    def spec(x):
        if isinstance(x, pl.BlockSpec):
            return x
        shape = x.shape
        return pl.BlockSpec(shape, lambda i, p: (0,) * len(shape))

    return pl.pallas_call(
        kernel,
        grid_spec=pltpu.PrefetchScalarGridSpec(
            num_scalar_prefetch=1,
            grid=(1,),
            in_specs=[spec(s) for _, s in args],
            out_specs=[spec(s) for _, s in outs],
            scratch_shapes=scratch,
        ),
        out_shape=[o for o, _ in outs],
        input_output_aliases=aliases or {},
        compiler_params=pltpu.CompilerParams(vmem_limit_bytes=LIMIT),
    )(place, *[a for a, _ in args])


def whole(x):
    return (x, x)


def part(x, index):
    shape = (HALF, *x.shape[1:])
    if callable(index):
        return (x, pl.BlockSpec(shape, lambda i, p: (index(p[0]),) + (0,) * (len(shape) - 1)))
    return (x, pl.BlockSpec(shape, lambda i, p: (index,) + (0,) * (len(shape) - 1)))


def smem(x):
    return (x, pl.BlockSpec(memory_space=pltpu.SMEM))


def untouched(x):
    return (x, pl.BlockSpec(memory_space=pl.ANY))


def shape(*s, dtype=F32):
    return jax.ShapeDtypeStruct(s, dtype)


def toward(box_count, nbr_count, receive):
    pairs = []
    for box in range(box_count):
        for place in range(nbr_count):
            step = 1 if (place < nbr_count // 2) == receive else -1
            other = (box + step) % box_count
            pairs.append((other * nbr_count + place, box * nbr_count + place))
    return pairs


def exchanged(x):
    return lax.all_to_all(x, "nbr", 0, 0, tiled=True).reshape(4, -1, *x.shape[1:])


def copies_kernel(place_ref, block_ref, first_ref, *rest):
    later, sem = rest[:3], rest[3]
    place = place_ref[0]
    copies = []
    for target in range(4):
        half = HALF * (1 if target < 2 else 0)
        copies.append((half, first_ref.at[pl.ds(target * HALF, HALF)]))
    for k in range(3):
        target = lax.rem(place + k + 1, 4)
        copies.append((HALF * half_of(target, 1), later[k]))
    copies = [
        pltpu.make_async_copy(block_ref.at[pl.ds(half, HALF)], out, sem.at[k])
        for k, (half, out) in enumerate(copies)
    ]
    for copy in copies:
        copy.start()
    for copy in copies:
        copy.wait()


def copies(place, self_block):
    anywhere = pl.BlockSpec(memory_space=pl.ANY)
    rest = self_block.shape[1:]
    return pl.pallas_call(
        copies_kernel,
        in_specs=[
            pl.BlockSpec(memory_space=pltpu.SMEM), pl.BlockSpec(memory_space=pltpu.VMEM),
        ],
        out_specs=[anywhere] * 4,
        out_shape=[shape(4 * HALF, *rest)] + [shape(HALF, *rest)] * 3,
        scratch_shapes=[pltpu.SemaphoreType.DMA((7,))],
        name="copies",
    )(place, self_block)


def whole_body(self_block, ordering, interp, near_band, pair_mask):
    boxes = ordering.shape[0]
    box_axis, nbr_axis = lax.axis_size("box"), lax.axis_size("nbr")
    place = lax.axis_index("nbr")
    low_side = place < nbr_axis // 2
    where = place.reshape(1)
    first, *later = copies(where, self_block)
    blocks_0 = exchanged(first)
    edge_start = jnp.where(low_side, 0, boxes - REACH)
    edge = lax.dynamic_slice_in_dim(near_band, edge_start, REACH, 0)
    edge_mask = jnp.where(low_side, pair_mask[:REACH], pair_mask[boxes - REACH :]).astype(F32)
    halo = lax.ppermute(
        edge * edge_mask[:, :, None, None, None],
        ("box", "nbr"),
        toward(box_axis, nbr_axis, True),
    )
    blocks_1 = []
    for k in range(3):
        turn = [(i, (i + k + 1) % nbr_axis) for i in range(nbr_axis)]
        blocks_1.append(lax.ppermute(later[k], "nbr", turn))
    wide = pltpu.VMEM((HALF, 2, PTS, PTS), BF)
    tail = pltpu.VMEM((HALF, RED, PTS), F32)
    extended = pltpu.VMEM((16, SKEL, PAIR), F32)
    all_blocks = pltpu.VMEM((4, HALF, SKEL, PTS), F32)
    all_rows = pltpu.VMEM((HALF, 2, 2, SKEL, PTS), F32)
    some_interp = pltpu.VMEM((HALF, SKEL, RED), F32)
    kept_shape = shape(HALF, SKEL, PAIR)
    pair_shape = shape(HALF, 2, PTS, PTS, dtype=BF)
    inverse_shape = shape(boxes, ROWS, RED)
    couple_shape, own_shape = shape(boxes, 2, SKEL, PAIR), shape(boxes, SKEL, SKEL)

    def halves(x, chunk):
        return part(x, lambda p: half_of(p, chunk))

    inverse, z, s, inv, skel, side = call(
        factor_kernel, where,
        [whole(ordering), untouched(interp), untouched(blocks_0)],
        [
            halves(inverse_shape, 0), whole(pair_shape), whole(pair_shape),
            whole(shape(HALF, 8, PTS)), whole(shape(HALF, SKEL, PTS)),
            whole(shape(HALF, PTS, PAIR)),
        ],
        [all_blocks, some_interp, wide, wide, tail, pltpu.SemaphoreType.DMA((2,))],
    )
    couple, own, kept, leaving = call(
        edge_kernel, where,
        [
            smem(pair_mask), untouched(near_band), untouched(halo), whole(z), whole(s), whole(inv),
            whole(skel), whole(side),
        ],
        [
            halves(couple_shape, 0), halves(own_shape, 0), whole(kept_shape), whole(kept_shape),
        ],
        [all_rows, extended, pltpu.SemaphoreType.DMA((8,))],
    )
    came = lax.ppermute(leaving, ("box", "nbr"), toward(box_axis, nbr_axis, False))
    red_inverse, couplings, own, total = call(
        inner_kernel, where,
        [
            smem(pair_mask), whole(ordering), untouched(interp), untouched(near_band),
            untouched(self_block), *[untouched(b) for b in blocks_1], whole(kept),
            untouched(inverse), untouched(couple), untouched(own),
        ],
        [
            halves(inverse_shape, 1), halves(couple_shape, 1), halves(own_shape, 1),
            whole(kept_shape),
        ],
        [
            all_blocks, some_interp, all_rows, wide, wide, wide, wide, tail, extended,
            pltpu.SemaphoreType.DMA((13,)),
        ],
        {10: 0, 11: 1, 12: 2},
    )
    lane_left = lax.broadcasted_iota(jnp.int32, (1, 1, PAIR), 2) < SKEL
    total = total + jnp.where(lane_left == low_side, came, 0.0)
    flat = total.reshape(HALF * SKEL, PAIR)
    gathered = exchanged(jnp.concatenate([flat] * 4)).sum(axis=0).reshape(HALF, SKEL, PAIR)
    update = jnp.concatenate([gathered[:, :, :SKEL], gathered[:, :, SKEL:]], axis=0)
    return own - update, red_inverse, couplings


def solution(mesh):
    placed = (
        P("box", "nbr", None),
        P("box", None),
        P("box", None, None),
        P("box", "nbr", None, None, None),
        P("box", "nbr"),
    )
    return jax.shard_map(
        whole_body,
        mesh=mesh,
        in_specs=placed,
        out_specs=(P("box", None, None), P("box", "nbr", None), P("box", "nbr", None, None)),
        check_vma=False,
    )
```

profile of v0, /device:TPU:1, one launch (start us, length us, event | category | flops | bytes accessed | tf_op | source)
XLA Modules:
  0.0 70.3 jit_solution(8743851263965709582)
XLA Ops:
  0.6 0.8 %select_convert_fusion = f32[4,2]{0,1:T(2,128)S(1)} fusion(s32[8,2]{0,1:T(2,128)} %param.9, pred[]{:T(512)S(6)} %lt.15), kind=kLoop, calls=%fused_computation.5 | loop fusion | flops 16 | bytes 97 | tf_op jit(solution)/shard_map/convert_element_type | solution.py:381
  1.5 0.1 copy.11
  1.6 2.4 %dynamic-slice_multiply_fusion = f32[4,2,2,64,256]{4,3,2,1,0:T(8,128)} fusion(f32[8,2,2,64,256]{4,3,2,1,0:T(8,128)} %near_ref.3, s32[]{:T(128)S(6)} %select_n.17, f32[4,2]{1,0:T(4,128)S(1)} %copy.11), kind=kLoop, calls=%fused_computation | loop fusion | flops 262144 | bytes 2097188 | tf_op jit(solution)/shard_map/mul | solution.py:383
  4.0 8.7 %collective-permute-start.3 = (f32[4,2,2,64,256]{4,3,2,1,0:T(8,128)}, f32[4,2,2,64,256]{4,3,2,1,0:T(8,128)}, u32[]{:S(2)}, u32[]{:S(2)}) collective-permute-start(f32[4,2,2,64,256]{4,3,2,1,0:T(8,128)} %dynamic-slice_multiply_fusion), channel_id=1, source_target_pairs={{4,0},{5,1},{510,2},{511,3},{8,4},{9,5},{2,6},{3,7},{12,8},{13,9},... | collective-permute-start | bytes 3145736 | tf_op jit(solution)/shard_map/ppermute | solution.py:382
  12.7 0.0 copy-start
  12.7 2.5 %copies.1 = (f32[16,64,256]{2,1,0:T(8,128)}, f32[4,64,256]{2,1,0:T(8,128)}, f32[4,64,256]{2,1,0:T(8,128)}, f32[4,64,256]{2,1,0:T(8,128)}) custom-call(s32[1]{0:T(128)} %bitcast.place_ref, f32[8,64,256]{2,1,0:T(8,128)} %block_ref.3), custom_call_target="tpu_custom_call" | custom-call | tf_op jit(solution)/shard_map/copies/pallas_call | solution.py:359
  15.2 3.5 %all-to-all-start = ((f32[16,64,256]{2,1,0:T(8,128)}), f32[16,64,256]{2,1,0:T(8,128)S(1)}, u32[]{:S(2)}, u32[]{:S(2)}) async-start(f32[16,64,256]{2,1,0:T(8,128)} %get-tuple-element.24), calls=%async_computation | async-start | bytes 2097152 | tf_op jit(solution)/shard_map/all_to_all | solution.py:333
  18.7 3.3 %collective-permute-start = (f32[4,64,256]{2,1,0:T(8,128)}, f32[4,64,256]{2,1,0:T(8,128)S(1)}, u32[]{:S(2)}, u32[]{:S(2)}) collective-permute-start(f32[4,64,256]{2,1,0:T(8,128)} %get-tuple-element.21), channel_id=1, source_target_pairs={{0,1},{1,2},{2,3},{3,0},{4,5},{5,6},{6,7},{7,4},{8,9},{9,10},{10,1... | collective-permute-start | bytes 786440 | tf_op jit(solution)/shard_map/ppermute | solution.py:390
  22.1 4.3 %collective-permute-start.1 = (f32[4,64,256]{2,1,0:T(8,128)}, f32[4,64,256]{2,1,0:T(8,128)}, u32[]{:S(2)}, u32[]{:S(2)}) collective-permute-start(f32[4,64,256]{2,1,0:T(8,128)} %get-tuple-element.22), channel_id=1, source_target_pairs={{0,2},{1,3},{2,0},{3,1},{4,6},{5,7},{6,4},{7,5},{8,10},{9,11},{10,... | collective-permute-start | bytes 786440 | tf_op jit(solution)/shard_map/ppermute | solution.py:390
  26.4 3.1 %collective-permute-start.2 = (f32[4,64,256]{2,1,0:T(8,128)}, f32[4,64,256]{2,1,0:T(8,128)}, u32[]{:S(2)}, u32[]{:S(2)}) collective-permute-start(f32[4,64,256]{2,1,0:T(8,128)} %get-tuple-element.23), channel_id=1, source_target_pairs={{0,3},{1,0},{2,1},{3,2},{4,7},{5,4},{6,5},{7,6},{8,11},{9,8},{10,9... | collective-permute-start | bytes 786440 | tf_op jit(solution)/shard_map/ppermute | solution.py:390
  29.5 0.0 copy-done.5
  29.5 0.1 copy.13.mask_ref
  29.6 0.0 all-to-all-done
  29.6 0.0 copy-done.4
  29.6 1.0 %copy-done.1 = f32[8,64,192]{2,1,0:T(8,128)S(1)} copy-done((f32[8,64,192]{2,1,0:T(8,128)S(1)}, f32[8,64,192]{2,1,0:T(8,128)}, u32[]{:S(2)}) %copy-start.1) | copy-done | bytes 393240
  30.6 3.9 %shard_map.76 = (f32[8,48,192]{2,1,0:T(8,128)}, bf16[4,2,256,256]{3,2,1,0:T(8,128)(2,1)S(1)}, bf16[4,2,256,256]{3,2,1,0:T(8,128)(2,1)S(1)}, f32[4,8,256]{2,1,0:T...) custom-call(s32[1]{0:T(128)} %bitcast.place_ref, s32[8,256]{1,0:T(8,128)S(1)} %copy-done.4, ...), custom_call_target="tpu_custom_call" | custom-call | tf_op jit(solution)/shard_map/pallas_call | solution.py:284
  34.5 0.0 collective-permute-done.3.halo_ref
  34.5 0.0 copy-done
  34.5 0.0 copy-start.2
  34.5 0.0 copy-start.3
  34.6 4.3 %shard_map.77 = (f32[8,2,64,128]{3,2,1,0:T(8,128)}, f32[8,64,64]{2,1,0:T(8,128)S(1)}, f32[4,64,128]{2,1,0:T(8,128)S(1)}, f32[4,64,128]{2,1,0:T(8,128)S(1)}) custom-call(s32[1]{0:T(128)} %bitcast.place_ref, s32[8,2]{1,0:T(8,128)S(1)} %copy.13.mask_ref, f32[8,2,2,64,256]{4,3,2,1,0:T(8,128)S(1)} %copy-done, ...), custom_call_target="tpu_custom_call" | custom-call | tf_op jit(solution)/shard_map/pallas_call | solution.py:284
  38.9 3.9 %collective-permute-start.4 = (f32[4,64,128]{2,1,0:T(8,128)S(1)}, f32[4,64,128]{2,1,0:T(8,128)S(1)}, u32[]{:S(2)}, u32[]{:S(2)}) collective-permute-start(f32[4,64,128]{2,1,0:T(8,128)S(1)} %get-tuple-element.36), channel_id=1, source_target_pairs={{508,0},{509,1},{6,2},{7,3},{0,4},{1,5},{10,6},{11,7},{4,8},{5,9},... | collective-permute-start | bytes 393224 | tf_op jit(solution)/shard_map/ppermute | solution.py:426
  42.8 0.0 collective-permute-done.came_1
  42.8 0.0 collective-permute-done.1.came_2
  42.8 0.0 collective-permute-done.2.came_3
  42.8 0.0 copy-done.2
  42.8 0.0 copy-done.3
  42.8 7.4 %shard_map.78 = (f32[8,48,192]{2,1,0:T(8,128)}, f32[8,2,64,128]{3,2,1,0:T(8,128)}, f32[8,64,64]{2,1,0:T(8,128)S(1)}, f32[4,64,128]{2,1,0:T(8,128)S(1)}) custom-call(s32[1]{0:T(128)} %bitcast.place_ref, s32[8,2]{1,0:T(8,128)S(1)} %copy.13.mask_ref, s32[8,256]{1,0:T(8,128)S(1)} %copy-done.4, ...), custom_call_target="tpu_custom_call", output_to_operand_aliasing={{0}: (10, {}), {1}: (11, {}), {2}: (12, {})} | custom-call | tf_op jit(solution)/shard_map/pallas_call | solution.py:284
  50.2 2.4 %collective-permute-done.4 = f32[4,64,128]{2,1,0:T(8,128)S(1)} collective-permute-done((f32[4,64,128]{2,1,0:T(8,128)S(1)}, f32[4,64,128]{2,1,0:T(8,128)S(1)}, u32[]{:S(2)}, u32[]{:S(2)}) %collective-permute-start.4) | collective-permute-done | bytes 131104 | tf_op jit(solution)/shard_map/ppermute | solution.py:426
  52.6 16.8 %all_to_all.14 = f32[4,256,128]{2,1,0:T(8,128)S(1)} all-to-all(f32[4,256,128]{2,1,0:T(8,128)S(1)} %bitcast.6), channel_id=1, replica_groups=mesh['box'=128,'nbr'=4] {'nbr'}, dimensions={0} | all-to-all | bytes 1048576 | tf_op jit(solution)/shard_map/all_to_all | solution.py:333
  69.5 0.1 fusion
  69.6 0.7 %maximum_subtract_fusion = f32[8,64,64]{2,1,0:T(8,128)} fusion(f32[8,64,64]{2,1,0:T(8,128)S(1)} %get-tuple-element.34, f32[4,64,64]{2,1,0:T(8,128)S(1)} %get-tuple-element.40, f32[4,64,64]{2,1,0:T(8,128)S(1)} %get-tuple-element.39), kind=kLoop, calls=%fused_computation.2 | loop fusion | flops 65536 | bytes 393216 | tf_op jit(solution)/shard_map/sub | solution.py:449
  (7 shorter events, 0.1 us)
Async XLA Ops:
  1.6 27.9 %copy-start.5 = (s32[8,2]{0,1:T(2,128)S(1)}, s32[8,2]{0,1:T(2,128)}, u32[]{:S(2)}) copy-start(s32[8,2]{0,1:T(2,128)} %param.9) | copy-start | bytes 196
  1.6 28.0 %copy-start.4 = (s32[8,256]{1,0:T(8,128)S(1)}, s32[8,256]{1,0:T(8,128)}, u32[]{:S(2)}) copy-start(s32[8,256]{1,0:T(8,128)} %order_ref.3) | copy-start | bytes 24580
  4.0 30.5 %collective-permute-start.3 = (f32[4,2,2,64,256]{4,3,2,1,0:T(8,128)}, f32[4,2,2,64,256]{4,3,2,1,0:T(8,128)}, u32[]{:S(2)}, u32[]{:S(2)}) collective-permute-start(f32[4,2,2,64,256]{4,3,2,1,0:T(8,128)} %dynamic-slice_multiply_fusion), channel_id=1, source_target_pairs={{4,0},{5,1},{510,2},{511,3},{8,4},{9,5},{2,6},{3,7},{12,8},{13,9},... | collective-permute-start | bytes 3145736 | tf_op jit(solution)/shard_map/ppermute | solution.py:382
  12.7 21.8 %copy-start = (f32[8,2,2,64,256]{4,3,2,1,0:T(8,128)S(1)}, f32[8,2,2,64,256]{4,3,2,1,0:T(8,128)}, u32[]{:S(2)}) copy-start(f32[8,2,2,64,256]{4,3,2,1,0:T(8,128)} %near_ref.3) | copy-start | bytes 6291460
  15.2 14.4 %all-to-all-start = ((f32[16,64,256]{2,1,0:T(8,128)}), f32[16,64,256]{2,1,0:T(8,128)S(1)}, u32[]{:S(2)}, u32[]{:S(2)}) async-start(f32[16,64,256]{2,1,0:T(8,128)} %get-tuple-element.24), calls=%async_computation | async-start | bytes 2097152 | tf_op jit(solution)/shard_map/all_to_all | solution.py:333
  18.7 24.0 %collective-permute-start = (f32[4,64,256]{2,1,0:T(8,128)}, f32[4,64,256]{2,1,0:T(8,128)S(1)}, u32[]{:S(2)}, u32[]{:S(2)}) collective-permute-start(f32[4,64,256]{2,1,0:T(8,128)} %get-tuple-element.21), channel_id=1, source_target_pairs={{0,1},{1,2},{2,3},{3,0},{4,5},{5,6},{6,7},{7,4},{8,9},{9,10},{10,1... | collective-permute-start | bytes 786440 | tf_op jit(solution)/shard_map/ppermute | solution.py:390
  22.1 20.7 %collective-permute-start.1 = (f32[4,64,256]{2,1,0:T(8,128)}, f32[4,64,256]{2,1,0:T(8,128)}, u32[]{:S(2)}, u32[]{:S(2)}) collective-permute-start(f32[4,64,256]{2,1,0:T(8,128)} %get-tuple-element.22), channel_id=1, source_target_pairs={{0,2},{1,3},{2,0},{3,1},{4,6},{5,7},{6,4},{7,5},{8,10},{9,11},{10,... | collective-permute-start | bytes 786440 | tf_op jit(solution)/shard_map/ppermute | solution.py:390
  26.4 16.4 %collective-permute-start.2 = (f32[4,64,256]{2,1,0:T(8,128)}, f32[4,64,256]{2,1,0:T(8,128)}, u32[]{:S(2)}, u32[]{:S(2)}) collective-permute-start(f32[4,64,256]{2,1,0:T(8,128)} %get-tuple-element.23), channel_id=1, source_target_pairs={{0,3},{1,0},{2,1},{3,2},{4,7},{5,4},{6,5},{7,6},{8,11},{9,8},{10,9... | collective-permute-start | bytes 786440 | tf_op jit(solution)/shard_map/ppermute | solution.py:390
  29.6 1.0 %copy-start.1 = (f32[8,64,192]{2,1,0:T(8,128)S(1)}, f32[8,64,192]{2,1,0:T(8,128)}, u32[]{:S(2)}) copy-start(f32[8,64,192]{2,1,0:T(8,128)} %interp_ref.3) | copy-start | bytes 1179652
  34.5 8.3 %copy-start.2 = (f32[8,64,192]{2,1,0:T(8,128)S(1)}, f32[8,64,192]{2,1,0:T(8,128)}, u32[]{:S(2)}) copy-start(f32[8,64,192]{2,1,0:T(8,128)} %interp_ref.3) | copy-start | bytes 1179652
  34.5 8.3 %copy-start.3 = (f32[8,64,256]{2,1,0:T(8,128)S(1)}, f32[8,64,256]{2,1,0:T(8,128)}, u32[]{:S(2)}) copy-start(f32[8,64,256]{2,1,0:T(8,128)} %block_ref.3) | copy-start | bytes 1572868
  38.9 13.7 %collective-permute-start.4 = (f32[4,64,128]{2,1,0:T(8,128)S(1)}, f32[4,64,128]{2,1,0:T(8,128)S(1)}, u32[]{:S(2)}, u32[]{:S(2)}) collective-permute-start(f32[4,64,128]{2,1,0:T(8,128)S(1)} %get-tuple-element.36), channel_id=1, source_target_pairs={{508,0},{509,1},{6,2},{7,3},{0,4},{1,5},{10,6},{11,7},{4,8},{5,9},... | collective-permute-start | bytes 393224 | tf_op jit(solution)/shard_map/ppermute | solution.py:426
where the time goes:
time: 70.8 us; the launch traced here: 70.3 us
  starting transfers between devices  26.9 us (38%)
  Pallas kernels  18 us (25%)
  blocking collectives  16.8 us (24%)
  other arithmetic  4.07 us (6%)
  waiting for transfers between devices  2.39 us (3%)
  local copies, waits for them, and re-layouts  1.34 us (2%)
  between operations  0.84 us (1%)
    all_to_all x1, blocking collectives, exchanged(): lax.all_to_all(x, 'nbr', 0, 0, tiled=True).reshape(4, -1, *x.shape[1:])  16.8 us
    pallas_call x3, Pallas kernels, call(): pl.pallas_call(kernel, grid_spec=pltpu.PrefetchScalarGridSpec(num_scalar_...  15.6 us
    ppermute x3, starting transfers between devices, whole_body(): blocks_1.append(lax.ppermute(later[k], 'nbr', turn))  10.7 us
    ppermute x1, starting transfers between devices, whole_body(): lax.ppermute(edge * edge_mask[:, :, None, None, None], ('box', 'nbr'), to...  8.74 us
    ppermute x1, starting transfers between devices, whole_body(): lax.ppermute(leaving, ('box', 'nbr'), toward(box_axis, nbr_axis, False))  3.88 us
    all_to_all x1, starting transfers between devices, exchanged(): lax.all_to_all(x, 'nbr', 0, 0, tiled=True).reshape(4, -1, *x.shape[1:])  3.53 us
    pallas_call x1, Pallas kernels, copies(): pl.pallas_call(copies_kernel, in_specs=[pl.BlockSpec(memory_space=pltpu.S...  2.45 us
    mul x1, other arithmetic, whole_body(): edge * edge_mask[:, :, None, None, None]  2.41 us
  transfers between devices with their start and end apart: 6, of which 1 were waited for; matrix products, arithmetic and copies ran while one was open for 0% of the time, Pallas kernels for 26%

commit v1 on v0

--- a/solution.py
+++ b/solution.py
@@ -62,40 +62,21 @@
             zt_ref[k, level] = z.T.astype(BF)
 
 
-def source_of(box, place, slot):
-    source = box - slot_offset(place, slot)
-    inside = jnp.logical_and(source >= 0, source < 2 * HALF)
-    return source, inside, jnp.clip(source, 0, 2 * HALF - 1)
-
-
-def fetch(boxes, place, near_ref, halo_ref, rows_ref, sem):
-    waits = []
-    for k, box in enumerate(boxes):
-        for slot in range(2):
-            source, inside, local = source_of(box, place, slot)
-            to = rows_ref.at[k, slot]
-            flag = sem.at[2 * k + slot]
-            near = pltpu.make_async_copy(near_ref.at[local, slot], to, flag)
-            waits.append(near)
-            if halo_ref is None:
-                near.start()
-            else:
-                remote = jnp.where(source >= 2 * HALF, source - 2 * HALF, source + HALF)
-                remote = jnp.clip(remote, 0, HALF - 1)
-                far = pltpu.make_async_copy(halo_ref.at[remote, slot], to, flag)
-                pl.when(inside)(near.start)
-                pl.when(jnp.logical_not(inside))(far.start)
-    return waits
-
-
-def meet(boxes, place, mask_ref, rows_ref, z_ref):
+def meet(boxes, place, mask_ref, near_ref, halo_ref, z_ref):
     g, nt = [], []
     for k, box in enumerate(boxes):
         rows = []
         for slot in range(2):
-            _, inside, local = source_of(box, place, slot)
-            weight = jnp.where(inside, mask_ref[local, slot], 1).astype(F32)
-            rows.append(rows_ref[k, slot] * weight)
+            source = box - slot_offset(place, slot)
+            inside = jnp.logical_and(source >= 0, source < 2 * HALF)
+            local = jnp.clip(source, 0, 2 * HALF - 1)
+            weight = jnp.where(inside, mask_ref[local, slot], 0).astype(F32)
+            row = near_ref[local, slot] * weight
+            if halo_ref is not None:
+                remote = jnp.where(source >= 2 * HALF, source - 2 * HALF, source + HALF)
+                remote = jnp.clip(remote, 0, HALF - 1)
+                row = row + halo_ref[remote, slot] * jnp.where(inside, 0, 1).astype(F32)
+            rows.append(row)
         stacked = jnp.concatenate([rows[0][0], rows[1][0], rows[0][1], rows[1][1]], axis=0)
         done = dot3(split(stacked), (z_ref[k, 0], z_ref[k, 1]))
         g.append(done[:PAIR])
@@ -229,14 +210,12 @@
 
 def edge_kernel(
     place_ref, mask_ref, near_ref, halo_ref, z_ref, s_ref, inv_ref, skel_ref, side_ref,
-    couple_ref, own_ref, kept_ref, leaving_ref, rows_ref, extended, sem,
+    couple_ref, own_ref, kept_ref, leaving_ref, extended,
 ):
     place = place_ref[0]
     boxes = boxes_of(place, 0)
-    waits = fetch(boxes, place, near_ref, halo_ref, rows_ref, sem)
     extended[...] = jnp.zeros_like(extended)
-    ended(waits)
-    g, nt = meet(boxes, place, mask_ref, rows_ref, z_ref)
+    g, nt = meet(boxes, place, mask_ref, near_ref, halo_ref, z_ref)
     inv = [inv_ref[k, :1] for k in range(HALF)]
     skel = [skel_ref[k] for k in range(HALF)]
     side = [side_ref[k] for k in range(HALF)]
@@ -252,23 +231,21 @@
     place_ref, mask_ref, order_ref, interp_ref, near_ref, block_ref, came_1, came_2, came_3,
     kept_in, inverse_in, couple_in, own_in,
     inverse_ref, couple_ref, own_ref, total_ref,
-    blocks_ref, interp, rows_ref, z_ref, zt_ref, even, odd, tail, extended, sem,
+    blocks_ref, interp, z_ref, zt_ref, even, odd, tail, extended, sem,
 ):
     place = place_ref[0]
     boxes = boxes_of(place, 1)
-    text = started([pltpu.make_async_copy(half_rows(interp_ref, place, 1), interp, sem.at[8])])
+    text = started([pltpu.make_async_copy(half_rows(interp_ref, place, 1), interp, sem.at[4])])
     parts = started([
-        pltpu.make_async_copy(source, blocks_ref.at[lax.rem(place + 4 - k, 4)], sem.at[9 + k])
+        pltpu.make_async_copy(source, blocks_ref.at[lax.rem(place + 4 - k, 4)], sem.at[k])
         for k, source in enumerate([half_rows(block_ref, place, 1), came_1, came_2, came_3])
     ])
-    waits = fetch(boxes, place, near_ref, None, rows_ref, sem)
     extended[...] = jnp.zeros_like(extended)
     ended(text)
     choose(boxes, order_ref, interp, even, z_ref, zt_ref)
     ended(parts)
     inv, skel, side = factor(place, blocks_ref, z_ref, zt_ref, even, odd, tail, inverse_ref)
-    ended(waits)
-    g, nt = meet(boxes, place, mask_ref, rows_ref, z_ref)
+    g, nt = meet(boxes, place, mask_ref, near_ref, None, z_ref)
     left = finish(boxes, place, inv, skel, side, g, nt, odd, couple_ref, own_ref, extended)
     for k, value in enumerate(packed(extended, left)):
         total_ref[k] = value + kept_in[k]
@@ -392,7 +369,6 @@
     tail = pltpu.VMEM((HALF, RED, PTS), F32)
     extended = pltpu.VMEM((16, SKEL, PAIR), F32)
     all_blocks = pltpu.VMEM((4, HALF, SKEL, PTS), F32)
-    all_rows = pltpu.VMEM((HALF, 2, 2, SKEL, PTS), F32)
     some_interp = pltpu.VMEM((HALF, SKEL, RED), F32)
     kept_shape = shape(HALF, SKEL, PAIR)
     pair_shape = shape(HALF, 2, PTS, PTS, dtype=BF)
@@ -415,19 +391,19 @@
     couple, own, kept, leaving = call(
         edge_kernel, where,
         [
-            smem(pair_mask), untouched(near_band), untouched(halo), whole(z), whole(s), whole(inv),
+            smem(pair_mask), whole(near_band), whole(halo), whole(z), whole(s), whole(inv),
             whole(skel), whole(side),
         ],
         [
             halves(couple_shape, 0), halves(own_shape, 0), whole(kept_shape), whole(kept_shape),
         ],
-        [all_rows, extended, pltpu.SemaphoreType.DMA((8,))],
+        [extended],
     )
     came = lax.ppermute(leaving, ("box", "nbr"), toward(box_axis, nbr_axis, False))
     red_inverse, couplings, own, total = call(
         inner_kernel, where,
         [
-            smem(pair_mask), whole(ordering), untouched(interp), untouched(near_band),
+            smem(pair_mask), whole(ordering), untouched(interp), whole(near_band),
             untouched(self_block), *[untouched(b) for b in blocks_1], whole(kept),
             untouched(inverse), untouched(couple), untouched(own),
         ],
@@ -436,8 +412,8 @@
             whole(kept_shape),
         ],
         [
-            all_blocks, some_interp, all_rows, wide, wide, wide, wide, tail, extended,
-            pltpu.SemaphoreType.DMA((13,)),
+            all_blocks, some_interp, wide, wide, wide, wide, tail, extended,
+            pltpu.SemaphoreType.DMA((5,)),
         ],
         {10: 0, 11: 1, 12: 2},
     )

time: 70.8 us -> 68.5 us (0.968); the launches traced: 70.3 us -> 67.2 us
  blocking collectives: 16.8 us -> 14.4 us
  Pallas kernels: 18 us -> 16.1 us
  waiting for transfers between devices: 2.39 us -> 3.64 us
    all_to_all x1, blocking collectives: 16.8 us -> 14.4 us  [exchanged(): lax.all_to_all(x, 'nbr', 0, 0, tiled=True).reshape(4, -1, *x.shape[1:])]
    pallas_call x3, Pallas kernels: 15.6 us -> 13.6 us  [call(): pl.pallas_call(kernel, grid_spec=pltpu.PrefetchScalarGridSpec(num_scalar_...]
    ppermute x1, waiting for transfers between devices: 2.38 us -> 3.62 us  [whole_body(): lax.ppermute(leaving, ('box', 'nbr'), toward(box_axis, nbr_axis, False))]
  transfers between devices with their start and end apart: 6 -> 6, of which waited for: 1 -> 1; matrix products, arithmetic and copies ran while one was open for 0% -> 0% of each run, Pallas kernels for 26% -> 24%
where the time goes in v1:
time: 68.5 us; the launch traced here: 67.2 us
  starting transfers between devices  26.8 us (39%)
  Pallas kernels  16.1 us (24%)
  blocking collectives  14.4 us (21%)
  other arithmetic  4.07 us (6%)
  waiting for transfers between devices  3.64 us (5%)
  local copies, waits for them, and re-layouts  1.34 us (2%)
  between operations  0.83 us (1%)
    all_to_all x1, blocking collectives, exchanged(): lax.all_to_all(x, 'nbr', 0, 0, tiled=True).reshape(4, -1, *x.shape[1:])  14.4 us
    pallas_call x3, Pallas kernels, call(): pl.pallas_call(kernel, grid_spec=pltpu.PrefetchScalarGridSpec(num_scalar_...  13.6 us
    ppermute x3, starting transfers between devices, whole_body(): blocks_1.append(lax.ppermute(later[k], 'nbr', turn))  10.7 us
    ppermute x1, starting transfers between devices, whole_body(): lax.ppermute(edge * edge_mask[:, :, None, None, None], ('box', 'nbr'), to...  8.74 us
    ppermute x1, starting transfers between devices, whole_body(): lax.ppermute(leaving, ('box', 'nbr'), toward(box_axis, nbr_axis, False))  3.86 us
    ppermute x1, waiting for transfers between devices, whole_body(): lax.ppermute(leaving, ('box', 'nbr'), toward(box_axis, nbr_axis, False))  3.62 us
    all_to_all x1, starting transfers between devices, exchanged(): lax.all_to_all(x, 'nbr', 0, 0, tiled=True).reshape(4, -1, *x.shape[1:])  3.53 us
    pallas_call x1, Pallas kernels, copies(): pl.pallas_call(copies_kernel, in_specs=[pl.BlockSpec(memory_space=pltpu.S...  2.45 us
  transfers between devices with their start and end apart: 6, of which 1 were waited for; matrix products, arithmetic and copies ran while one was open for 0% of the time, Pallas kernels for 24%

profile of v1, /device:TPU:1, one launch (start us, length us, event | category | flops | bytes accessed | tf_op | source)
XLA Modules:
  0.0 67.2 jit_solution(16404528670049481483)
XLA Ops:
  0.6 0.8 %select_convert_fusion = f32[4,2]{0,1:T(2,128)S(1)} fusion(s32[8,2]{0,1:T(2,128)} %param.9, pred[]{:T(512)S(6)} %lt.15), kind=kLoop, calls=%fused_computation.5 | loop fusion | flops 16 | bytes 97 | tf_op jit(solution)/shard_map/convert_element_type | solution.py:358
  1.5 0.1 copy.11
  1.6 2.4 %dynamic-slice_multiply_fusion = f32[4,2,2,64,256]{4,3,2,1,0:T(8,128)} fusion(f32[8,2,2,64,256]{4,3,2,1,0:T(8,128)} %near_ref.3, s32[]{:T(128)S(6)} %select_n.17, f32[4,2]{1,0:T(4,128)S(1)} %copy.11), kind=kLoop, calls=%fused_computation | loop fusion | flops 262144 | bytes 2097188 | tf_op jit(solution)/shard_map/mul | solution.py:360
  4.0 8.7 %collective-permute-start.3 = (f32[4,2,2,64,256]{4,3,2,1,0:T(8,128)}, f32[4,2,2,64,256]{4,3,2,1,0:T(8,128)}, u32[]{:S(2)}, u32[]{:S(2)}) collective-permute-start(f32[4,2,2,64,256]{4,3,2,1,0:T(8,128)} %dynamic-slice_multiply_fusion), channel_id=1, source_target_pairs={{4,0},{5,1},{510,2},{511,3},{8,4},{9,5},{2,6},{3,7},{12,8},{13,9},... | collective-permute-start | bytes 3145736 | tf_op jit(solution)/shard_map/ppermute | solution.py:359
  12.7 0.0 copy-start
  12.7 2.5 %copies.1 = (f32[16,64,256]{2,1,0:T(8,128)}, f32[4,64,256]{2,1,0:T(8,128)}, f32[4,64,256]{2,1,0:T(8,128)}, f32[4,64,256]{2,1,0:T(8,128)}) custom-call(s32[1]{0:T(128)} %bitcast.place_ref, f32[8,64,256]{2,1,0:T(8,128)} %block_ref.3), custom_call_target="tpu_custom_call" | custom-call | tf_op jit(solution)/shard_map/copies/pallas_call | solution.py:336
  15.2 3.5 %all-to-all-start = ((f32[16,64,256]{2,1,0:T(8,128)}), f32[16,64,256]{2,1,0:T(8,128)S(1)}, u32[]{:S(2)}, u32[]{:S(2)}) async-start(f32[16,64,256]{2,1,0:T(8,128)} %get-tuple-element.24), calls=%async_computation | async-start | bytes 2097152 | tf_op jit(solution)/shard_map/all_to_all | solution.py:310
  18.7 3.3 %collective-permute-start = (f32[4,64,256]{2,1,0:T(8,128)}, f32[4,64,256]{2,1,0:T(8,128)S(1)}, u32[]{:S(2)}, u32[]{:S(2)}) collective-permute-start(f32[4,64,256]{2,1,0:T(8,128)} %get-tuple-element.21), channel_id=1, source_target_pairs={{0,1},{1,2},{2,3},{3,0},{4,5},{5,6},{6,7},{7,4},{8,9},{9,10},{10,1... | collective-permute-start | bytes 786440 | tf_op jit(solution)/shard_map/ppermute | solution.py:367
  22.1 4.3 %collective-permute-start.1 = (f32[4,64,256]{2,1,0:T(8,128)}, f32[4,64,256]{2,1,0:T(8,128)}, u32[]{:S(2)}, u32[]{:S(2)}) collective-permute-start(f32[4,64,256]{2,1,0:T(8,128)} %get-tuple-element.22), channel_id=1, source_target_pairs={{0,2},{1,3},{2,0},{3,1},{4,6},{5,7},{6,4},{7,5},{8,10},{9,11},{10,... | collective-permute-start | bytes 786440 | tf_op jit(solution)/shard_map/ppermute | solution.py:367
  26.4 3.1 %collective-permute-start.2 = (f32[4,64,256]{2,1,0:T(8,128)}, f32[4,64,256]{2,1,0:T(8,128)}, u32[]{:S(2)}, u32[]{:S(2)}) collective-permute-start(f32[4,64,256]{2,1,0:T(8,128)} %get-tuple-element.23), channel_id=1, source_target_pairs={{0,3},{1,0},{2,1},{3,2},{4,7},{5,4},{6,5},{7,6},{8,11},{9,8},{10,9... | collective-permute-start | bytes 786440 | tf_op jit(solution)/shard_map/ppermute | solution.py:367
  29.5 0.0 copy-done.5
  29.5 0.1 copy.13.mask_ref
  29.6 0.0 all-to-all-done
  29.6 0.0 copy-done.4
  29.6 1.0 %copy-done.1 = f32[8,64,192]{2,1,0:T(8,128)S(1)} copy-done((f32[8,64,192]{2,1,0:T(8,128)S(1)}, f32[8,64,192]{2,1,0:T(8,128)}, u32[]{:S(2)}) %copy-start.1) | copy-done | bytes 393240
  30.6 3.9 %shard_map.76 = (f32[8,48,192]{2,1,0:T(8,128)}, bf16[4,2,256,256]{3,2,1,0:T(8,128)(2,1)S(1)}, bf16[4,2,256,256]{3,2,1,0:T(8,128)(2,1)S(1)}, f32[4,8,256]{2,1,0:T...) custom-call(s32[1]{0:T(128)} %bitcast.place_ref, s32[8,256]{1,0:T(8,128)S(1)} %copy-done.4, ...), custom_call_target="tpu_custom_call" | custom-call | tf_op jit(solution)/shard_map/pallas_call | solution.py:261
  34.5 0.0 collective-permute-done.3.halo_ref
  34.5 0.0 copy-done
  34.5 0.0 copy-start.2
  34.5 0.0 copy-start.3
  34.6 3.6 %shard_map.77 = (f32[8,2,64,128]{3,2,1,0:T(8,128)}, f32[8,64,64]{2,1,0:T(8,128)S(1)}, f32[4,64,128]{2,1,0:T(8,128)S(1)}, f32[4,64,128]{2,1,0:T(8,128)S(1)}) custom-call(s32[1]{0:T(128)} %bitcast.place_ref, s32[8,2]{1,0:T(8,128)S(1)} %copy.13.mask_ref, f32[8,2,2,64,256]{4,3,2,1,0:T(8,128)S(1)} %copy-done, ...), custom_call_target="tpu_custom_call" | custom-call | tf_op jit(solution)/shard_map/pallas_call | solution.py:261
  38.2 3.9 %collective-permute-start.4 = (f32[4,64,128]{2,1,0:T(8,128)S(1)}, f32[4,64,128]{2,1,0:T(8,128)S(1)}, u32[]{:S(2)}, u32[]{:S(2)}) collective-permute-start(f32[4,64,128]{2,1,0:T(8,128)S(1)} %get-tuple-element.36), channel_id=1, source_target_pairs={{508,0},{509,1},{6,2},{7,3},{0,4},{1,5},{10,6},{11,7},{4,8},{5,9},... | collective-permute-start | bytes 393224 | tf_op jit(solution)/shard_map/ppermute | solution.py:402
  42.1 0.0 collective-permute-done.came_1
  42.1 0.0 collective-permute-done.1.came_2
  42.1 0.0 collective-permute-done.2.came_3
  42.1 0.0 copy-done.2
  42.1 0.0 copy-done.3
  42.1 6.1 %shard_map.78 = (f32[8,48,192]{2,1,0:T(8,128)}, f32[8,2,64,128]{3,2,1,0:T(8,128)}, f32[8,64,64]{2,1,0:T(8,128)S(1)}, f32[4,64,128]{2,1,0:T(8,128)S(1)}) custom-call(s32[1]{0:T(128)} %bitcast.place_ref, s32[8,2]{1,0:T(8,128)S(1)} %copy.13.mask_ref, s32[8,256]{1,0:T(8,128)S(1)} %copy-done.4, ...), custom_call_target="tpu_custom_call", output_to_operand_aliasing={{0}: (10, {}), {1}: (11, {}), {2}: (12, {})} | custom-call | tf_op jit(solution)/shard_map/pallas_call | solution.py:261
  48.2 3.6 %collective-permute-done.4 = f32[4,64,128]{2,1,0:T(8,128)S(1)} collective-permute-done((f32[4,64,128]{2,1,0:T(8,128)S(1)}, f32[4,64,128]{2,1,0:T(8,128)S(1)}, u32[]{:S(2)}, u32[]{:S(2)}) %collective-permute-start.4) | collective-permute-done | bytes 131104 | tf_op jit(solution)/shard_map/ppermute | solution.py:402
  51.9 14.4 %all_to_all.14 = f32[4,256,128]{2,1,0:T(8,128)S(1)} all-to-all(f32[4,256,128]{2,1,0:T(8,128)S(1)} %bitcast.6), channel_id=1, replica_groups=mesh['box'=128,'nbr'=4] {'nbr'}, dimensions={0} | all-to-all | bytes 1048576 | tf_op jit(solution)/shard_map/all_to_all | solution.py:310
  66.4 0.1 fusion
  66.5 0.7 %maximum_subtract_fusion = f32[8,64,64]{2,1,0:T(8,128)} fusion(f32[8,64,64]{2,1,0:T(8,128)S(1)} %get-tuple-element.34, f32[4,64,64]{2,1,0:T(8,128)S(1)} %get-tuple-element.40, f32[4,64,64]{2,1,0:T(8,128)S(1)} %get-tuple-element.39), kind=kLoop, calls=%fused_computation.2 | loop fusion | flops 65536 | bytes 393216 | tf_op jit(solution)/shard_map/sub | solution.py:425
  (7 shorter events, 0.1 us)
Async XLA Ops:
  1.6 27.9 %copy-start.5 = (s32[8,2]{0,1:T(2,128)S(1)}, s32[8,2]{0,1:T(2,128)}, u32[]{:S(2)}) copy-start(s32[8,2]{0,1:T(2,128)} %param.9) | copy-start | bytes 196
  1.6 28.0 %copy-start.4 = (s32[8,256]{1,0:T(8,128)S(1)}, s32[8,256]{1,0:T(8,128)}, u32[]{:S(2)}) copy-start(s32[8,256]{1,0:T(8,128)} %order_ref.3) | copy-start | bytes 24580
  4.0 30.5 %collective-permute-start.3 = (f32[4,2,2,64,256]{4,3,2,1,0:T(8,128)}, f32[4,2,2,64,256]{4,3,2,1,0:T(8,128)}, u32[]{:S(2)}, u32[]{:S(2)}) collective-permute-start(f32[4,2,2,64,256]{4,3,2,1,0:T(8,128)} %dynamic-slice_multiply_fusion), channel_id=1, source_target_pairs={{4,0},{5,1},{510,2},{511,3},{8,4},{9,5},{2,6},{3,7},{12,8},{13,9},... | collective-permute-start | bytes 3145736 | tf_op jit(solution)/shard_map/ppermute | solution.py:359
  12.7 21.8 %copy-start = (f32[8,2,2,64,256]{4,3,2,1,0:T(8,128)S(1)}, f32[8,2,2,64,256]{4,3,2,1,0:T(8,128)}, u32[]{:S(2)}) copy-start(f32[8,2,2,64,256]{4,3,2,1,0:T(8,128)} %near_ref.3) | copy-start | bytes 6291460
  15.2 14.4 %all-to-all-start = ((f32[16,64,256]{2,1,0:T(8,128)}), f32[16,64,256]{2,1,0:T(8,128)S(1)}, u32[]{:S(2)}, u32[]{:S(2)}) async-start(f32[16,64,256]{2,1,0:T(8,128)} %get-tuple-element.24), calls=%async_computation | async-start | bytes 2097152 | tf_op jit(solution)/shard_map/all_to_all | solution.py:310
  18.7 23.3 %collective-permute-start = (f32[4,64,256]{2,1,0:T(8,128)}, f32[4,64,256]{2,1,0:T(8,128)S(1)}, u32[]{:S(2)}, u32[]{:S(2)}) collective-permute-start(f32[4,64,256]{2,1,0:T(8,128)} %get-tuple-element.21), channel_id=1, source_target_pairs={{0,1},{1,2},{2,3},{3,0},{4,5},{5,6},{6,7},{7,4},{8,9},{9,10},{10,1... | collective-permute-start | bytes 786440 | tf_op jit(solution)/shard_map/ppermute | solution.py:367
  22.1 20.0 %collective-permute-start.1 = (f32[4,64,256]{2,1,0:T(8,128)}, f32[4,64,256]{2,1,0:T(8,128)}, u32[]{:S(2)}, u32[]{:S(2)}) collective-permute-start(f32[4,64,256]{2,1,0:T(8,128)} %get-tuple-element.22), channel_id=1, source_target_pairs={{0,2},{1,3},{2,0},{3,1},{4,6},{5,7},{6,4},{7,5},{8,10},{9,11},{10,... | collective-permute-start | bytes 786440 | tf_op jit(solution)/shard_map/ppermute | solution.py:367
  26.4 15.7 %collective-permute-start.2 = (f32[4,64,256]{2,1,0:T(8,128)}, f32[4,64,256]{2,1,0:T(8,128)}, u32[]{:S(2)}, u32[]{:S(2)}) collective-permute-start(f32[4,64,256]{2,1,0:T(8,128)} %get-tuple-element.23), channel_id=1, source_target_pairs={{0,3},{1,0},{2,1},{3,2},{4,7},{5,4},{6,5},{7,6},{8,11},{9,8},{10,9... | collective-permute-start | bytes 786440 | tf_op jit(solution)/shard_map/ppermute | solution.py:367
  29.6 1.0 %copy-start.1 = (f32[8,64,192]{2,1,0:T(8,128)S(1)}, f32[8,64,192]{2,1,0:T(8,128)}, u32[]{:S(2)}) copy-start(f32[8,64,192]{2,1,0:T(8,128)} %interp_ref.3) | copy-start | bytes 1179652
  34.5 7.6 %copy-start.2 = (f32[8,64,192]{2,1,0:T(8,128)S(1)}, f32[8,64,192]{2,1,0:T(8,128)}, u32[]{:S(2)}) copy-start(f32[8,64,192]{2,1,0:T(8,128)} %interp_ref.3) | copy-start | bytes 1179652
  34.5 7.6 %copy-start.3 = (f32[8,64,256]{2,1,0:T(8,128)S(1)}, f32[8,64,256]{2,1,0:T(8,128)}, u32[]{:S(2)}) copy-start(f32[8,64,256]{2,1,0:T(8,128)} %block_ref.3) | copy-start | bytes 1572868
  38.2 13.7 %collective-permute-start.4 = (f32[4,64,128]{2,1,0:T(8,128)S(1)}, f32[4,64,128]{2,1,0:T(8,128)S(1)}, u32[]{:S(2)}, u32[]{:S(2)}) collective-permute-start(f32[4,64,128]{2,1,0:T(8,128)S(1)} %get-tuple-element.36), channel_id=1, source_target_pairs={{508,0},{509,1},{6,2},{7,3},{0,4},{1,5},{10,6},{11,7},{4,8},{5,9},... | collective-permute-start | bytes 393224 | tf_op jit(solution)/shard_map/ppermute | solution.py:402

commit v2 on v1

--- a/solution.py
+++ b/solution.py
@@ -45,21 +45,23 @@
     return jnp.where(place < 2, 1 - chunk, chunk)
 
 
-def choose(boxes, order_ref, interp, mixer, z_ref, zt_ref):
+def choose(boxes, order_ref, interp, z_ref, zt_ref):
     unknown = lax.broadcasted_iota(jnp.int32, (PTS, PTS), 0)
-    upper = eye(RED, PTS).astype(BF)
-    nothing = jnp.zeros((RED, PTS), BF)
+    column = lax.broadcasted_iota(jnp.int32, (PTS, PTS), 1)
+    lane = lax.broadcasted_iota(jnp.int32, (1, PAIR), 1)
+    one, nothing = eye(SKEL, SKEL).astype(BF), jnp.zeros((SKEL, SKEL), BF)
     for k, box in enumerate(boxes):
-        low = jnp.concatenate([-interp[k], eye(SKEL, SKEL)], axis=1)
-        mixer[k, 0, :RED], mixer[k, 1, :RED] = upper, nothing
-        mixer[k, 0, RED:], mixer[k, 1, RED:] = split(low)
-    for k, box in enumerate(boxes):
-        order = pltpu.roll(order_ref[pl.ds(box, 1), :], RED, 1)
-        chooser = (unknown == order).astype(F32).astype(BF)
-        for level in range(2):
-            z = dot(chooser, mixer[k, level])
-            z_ref[k, level] = z.astype(BF)
-            zt_ref[k, level] = z.T.astype(BF)
+        order = order_ref[pl.ds(box, 1), :]
+        red = jnp.logical_and(unknown == pltpu.roll(order, RED, 1), column < RED).astype(F32)
+        twice = jnp.where(lane < SKEL, order[:, :PAIR], pltpu.roll(order, SKEL, 1)[:, :PAIR])
+        skel = (unknown[:, :PAIR] == twice).astype(F32).astype(BF)
+        high, low = split(-interp[k])
+        both = jnp.concatenate(
+            [jnp.concatenate([high, one], axis=1), jnp.concatenate([low, nothing], axis=1)], axis=0
+        )
+        z = red + dot(skel, both)
+        z_ref[k, 0], z_ref[k, 1] = split(z)
+        zt_ref[k, 0], zt_ref[k, 1] = split(z.T)
 
 
 def meet(boxes, place, mask_ref, near_ref, halo_ref, z_ref):
@@ -200,7 +202,7 @@
         pltpu.make_async_copy(first_ref, blocks_ref, sem.at[1]),
     ])
     ended(needs[:1])
-    choose(boxes_of(place, 0), order_ref, interp, even, z_ref, zt_ref)
+    choose(boxes_of(place, 0), order_ref, interp, z_ref, zt_ref)
     ended(needs[1:])
     inv, skel, side = factor(place, blocks_ref, z_ref, zt_ref, even, s_ref, tail, inverse_ref)
     for k in range(HALF):
@@ -242,7 +244,7 @@
     ])
     extended[...] = jnp.zeros_like(extended)
     ended(text)
-    choose(boxes, order_ref, interp, even, z_ref, zt_ref)
+    choose(boxes, order_ref, interp, z_ref, zt_ref)
     ended(parts)
     inv, skel, side = factor(place, blocks_ref, z_ref, zt_ref, even, odd, tail, inverse_ref)
     g, nt = meet(boxes, place, mask_ref, near_ref, None, z_ref)

time: 68.5 us -> 68.4 us (level)
  the two profiles are of different devices: /device:TPU:1 before, /device:TPU:2 now
where the time goes in v2:
time: 68.4 us; the launch traced here: 67.9 us
  starting transfers between devices  29.6 us (43%)
  Pallas kernels  15.9 us (23%)
  blocking collectives  10.2 us (15%)
  waiting for transfers between devices  5.87 us (9%)
  other arithmetic  4.07 us (6%)
  local copies, waits for them, and re-layouts  1.34 us (2%)
  between operations  0.82 us (1%)
    pallas_call x3, Pallas kernels, call(): pl.pallas_call(kernel, grid_spec=pltpu.PrefetchScalarGridSpec(num_scalar_...  13.5 us
    ppermute x1, starting transfers between devices, whole_body(): lax.ppermute(edge * edge_mask[:, :, None, None, None], ('box', 'nbr'), to...  13.3 us
    ppermute x3, starting transfers between devices, whole_body(): blocks_1.append(lax.ppermute(later[k], 'nbr', turn))  10.4 us
    all_to_all x1, blocking collectives, exchanged(): lax.all_to_all(x, 'nbr', 0, 0, tiled=True).reshape(4, -1, *x.shape[1:])  10.2 us
    all_to_all x1, waiting for transfers between devices, exchanged(): lax.all_to_all(x, 'nbr', 0, 0, tiled=True).reshape(4, -1, *x.shape[1:])  4.29 us
    all_to_all x1, starting transfers between devices, exchanged(): lax.all_to_all(x, 'nbr', 0, 0, tiled=True).reshape(4, -1, *x.shape[1:])  4.03 us
    pallas_call x1, Pallas kernels, copies(): pl.pallas_call(copies_kernel, in_specs=[pl.BlockSpec(memory_space=pltpu.S...  2.45 us
    mul x1, other arithmetic, whole_body(): edge * edge_mask[:, :, None, None, None]  2.41 us
  transfers between devices with their start and end apart: 6, of which 2 were waited for; matrix products, arithmetic and copies ran while one was open for 0% of the time, Pallas kernels for 23%

profile of v2, /device:TPU:2, one launch (start us, length us, event | category | flops | bytes accessed | tf_op | source)
XLA Modules:
  0.0 67.9 jit_solution(17764294001514714180)
XLA Ops:
  0.6 0.8 %select_convert_fusion = f32[4,2]{0,1:T(2,128)S(1)} fusion(s32[8,2]{0,1:T(2,128)} %param.9, pred[]{:T(512)S(6)} %lt.15), kind=kLoop, calls=%fused_computation.5 | loop fusion | flops 16 | bytes 97 | tf_op jit(solution)/shard_map/convert_element_type | solution.py:360
  1.5 0.1 copy.11
  1.6 2.4 %dynamic-slice_multiply_fusion = f32[4,2,2,64,256]{4,3,2,1,0:T(8,128)} fusion(f32[8,2,2,64,256]{4,3,2,1,0:T(8,128)} %near_ref.3, s32[]{:T(128)S(6)} %select_n.17, f32[4,2]{1,0:T(4,128)S(1)} %copy.11), kind=kLoop, calls=%fused_computation | loop fusion | flops 262144 | bytes 2097188 | tf_op jit(solution)/shard_map/mul | solution.py:362
  4.0 13.3 %collective-permute-start.3 = (f32[4,2,2,64,256]{4,3,2,1,0:T(8,128)}, f32[4,2,2,64,256]{4,3,2,1,0:T(8,128)}, u32[]{:S(2)}, u32[]{:S(2)}) collective-permute-start(f32[4,2,2,64,256]{4,3,2,1,0:T(8,128)} %dynamic-slice_multiply_fusion), channel_id=1, source_target_pairs={{4,0},{5,1},{510,2},{511,3},{8,4},{9,5},{2,6},{3,7},{12,8},{13,9},... | collective-permute-start | bytes 3145736 | tf_op jit(solution)/shard_map/ppermute | solution.py:361
  17.3 0.0 copy-start
  17.3 2.5 %copies.1 = (f32[16,64,256]{2,1,0:T(8,128)}, f32[4,64,256]{2,1,0:T(8,128)}, f32[4,64,256]{2,1,0:T(8,128)}, f32[4,64,256]{2,1,0:T(8,128)}) custom-call(s32[1]{0:T(128)} %bitcast.place_ref, f32[8,64,256]{2,1,0:T(8,128)} %block_ref.3), custom_call_target="tpu_custom_call" | custom-call | tf_op jit(solution)/shard_map/copies/pallas_call | solution.py:338
  19.7 4.0 %all-to-all-start = ((f32[16,64,256]{2,1,0:T(8,128)}), f32[16,64,256]{2,1,0:T(8,128)S(1)}, u32[]{:S(2)}, u32[]{:S(2)}) async-start(f32[16,64,256]{2,1,0:T(8,128)} %get-tuple-element.24), calls=%async_computation | async-start | bytes 2097152 | tf_op jit(solution)/shard_map/all_to_all | solution.py:312
  23.8 3.4 %collective-permute-start = (f32[4,64,256]{2,1,0:T(8,128)}, f32[4,64,256]{2,1,0:T(8,128)S(1)}, u32[]{:S(2)}, u32[]{:S(2)}) collective-permute-start(f32[4,64,256]{2,1,0:T(8,128)} %get-tuple-element.21), channel_id=1, source_target_pairs={{0,1},{1,2},{2,3},{3,0},{4,5},{5,6},{6,7},{7,4},{8,9},{9,10},{10,1... | collective-permute-start | bytes 786440 | tf_op jit(solution)/shard_map/ppermute | solution.py:369
  27.1 2.6 %collective-permute-start.1 = (f32[4,64,256]{2,1,0:T(8,128)}, f32[4,64,256]{2,1,0:T(8,128)}, u32[]{:S(2)}, u32[]{:S(2)}) collective-permute-start(f32[4,64,256]{2,1,0:T(8,128)} %get-tuple-element.22), channel_id=1, source_target_pairs={{0,2},{1,3},{2,0},{3,1},{4,6},{5,7},{6,4},{7,5},{8,10},{9,11},{10,... | collective-permute-start | bytes 786440 | tf_op jit(solution)/shard_map/ppermute | solution.py:369
  29.7 4.5 %collective-permute-start.2 = (f32[4,64,256]{2,1,0:T(8,128)}, f32[4,64,256]{2,1,0:T(8,128)}, u32[]{:S(2)}, u32[]{:S(2)}) collective-permute-start(f32[4,64,256]{2,1,0:T(8,128)} %get-tuple-element.23), channel_id=1, source_target_pairs={{0,3},{1,0},{2,1},{3,2},{4,7},{5,4},{6,5},{7,6},{8,11},{9,8},{10,9... | collective-permute-start | bytes 786440 | tf_op jit(solution)/shard_map/ppermute | solution.py:369
  34.2 0.0 copy-done.5
  34.2 0.1 copy.13.mask_ref
  34.3 4.3 %all-to-all-done = f32[16,64,256]{2,1,0:T(8,128)S(1)} async-done(((f32[16,64,256]{2,1,0:T(8,128)}), f32[16,64,256]{2,1,0:T(8,128)S(1)}, u32[]{:S(2)}, u32[]{:S(2)}) %all-to-all-start) | async-done | bytes 1048608 | tf_op jit(solution)/shard_map/all_to_all | solution.py:312
  38.6 0.0 copy-done.4
  38.6 1.0 %copy-done.1 = f32[8,64,192]{2,1,0:T(8,128)S(1)} copy-done((f32[8,64,192]{2,1,0:T(8,128)S(1)}, f32[8,64,192]{2,1,0:T(8,128)}, u32[]{:S(2)}) %copy-start.1) | copy-done | bytes 393240
  39.6 3.8 %shard_map.76 = (f32[8,48,192]{2,1,0:T(8,128)}, bf16[4,2,256,256]{3,2,1,0:T(8,128)(2,1)S(1)}, bf16[4,2,256,256]{3,2,1,0:T(8,128)(2,1)S(1)}, f32[4,8,256]{2,1,0:T...) custom-call(s32[1]{0:T(128)} %bitcast.place_ref, s32[8,256]{1,0:T(8,128)S(1)} %copy-done.4, ...), custom_call_target="tpu_custom_call" | custom-call | tf_op jit(solution)/shard_map/pallas_call | solution.py:263
  43.5 0.0 collective-permute-done.3.halo_ref
  43.5 0.0 copy-done
  43.5 0.0 copy-start.2
  43.5 0.0 copy-start.3
  43.5 3.6 %shard_map.77 = (f32[8,2,64,128]{3,2,1,0:T(8,128)}, f32[8,64,64]{2,1,0:T(8,128)S(1)}, f32[4,64,128]{2,1,0:T(8,128)S(1)}, f32[4,64,128]{2,1,0:T(8,128)S(1)}) custom-call(s32[1]{0:T(128)} %bitcast.place_ref, s32[8,2]{1,0:T(8,128)S(1)} %copy.13.mask_ref, f32[8,2,2,64,256]{4,3,2,1,0:T(8,128)S(1)} %copy-done, ...), custom_call_target="tpu_custom_call" | custom-call | tf_op jit(solution)/shard_map/pallas_call | solution.py:263
  47.1 1.9 %collective-permute-start.4 = (f32[4,64,128]{2,1,0:T(8,128)S(1)}, f32[4,64,128]{2,1,0:T(8,128)S(1)}, u32[]{:S(2)}, u32[]{:S(2)}) collective-permute-start(f32[4,64,128]{2,1,0:T(8,128)S(1)} %get-tuple-element.36), channel_id=1, source_target_pairs={{508,0},{509,1},{6,2},{7,3},{0,4},{1,5},{10,6},{11,7},{4,8},{5,9},... | collective-permute-start | bytes 393224 | tf_op jit(solution)/shard_map/ppermute | solution.py:404
  49.1 0.0 collective-permute-done.came_1
  49.1 0.0 collective-permute-done.1.came_2
  49.1 0.0 collective-permute-done.2.came_3
  49.1 0.0 copy-done.2
  49.1 0.0 copy-done.3
  49.1 6.0 %shard_map.78 = (f32[8,48,192]{2,1,0:T(8,128)}, f32[8,2,64,128]{3,2,1,0:T(8,128)}, f32[8,64,64]{2,1,0:T(8,128)S(1)}, f32[4,64,128]{2,1,0:T(8,128)S(1)}) custom-call(s32[1]{0:T(128)} %bitcast.place_ref, s32[8,2]{1,0:T(8,128)S(1)} %copy.13.mask_ref, s32[8,256]{1,0:T(8,128)S(1)} %copy-done.4, ...), custom_call_target="tpu_custom_call", output_to_operand_aliasing={{0}: (10, {}), {1}: (11, {}), {2}: (12, {})} | custom-call | tf_op jit(solution)/shard_map/pallas_call | solution.py:263
  55.2 1.6 %collective-permute-done.4 = f32[4,64,128]{2,1,0:T(8,128)S(1)} collective-permute-done((f32[4,64,128]{2,1,0:T(8,128)S(1)}, f32[4,64,128]{2,1,0:T(8,128)S(1)}, u32[]{:S(2)}, u32[]{:S(2)}) %collective-permute-start.4) | collective-permute-done | bytes 131104 | tf_op jit(solution)/shard_map/ppermute | solution.py:404
  56.8 10.2 %all_to_all.14 = f32[4,256,128]{2,1,0:T(8,128)S(1)} all-to-all(f32[4,256,128]{2,1,0:T(8,128)S(1)} %bitcast.6), channel_id=1, replica_groups=mesh['box'=128,'nbr'=4] {'nbr'}, dimensions={0} | all-to-all | bytes 1048576 | tf_op jit(solution)/shard_map/all_to_all | solution.py:312
  67.0 0.1 fusion
  67.1 0.7 %maximum_subtract_fusion = f32[8,64,64]{2,1,0:T(8,128)} fusion(f32[8,64,64]{2,1,0:T(8,128)S(1)} %get-tuple-element.34, f32[4,64,64]{2,1,0:T(8,128)S(1)} %get-tuple-element.40, f32[4,64,64]{2,1,0:T(8,128)S(1)} %get-tuple-element.39), kind=kLoop, calls=%fused_computation.2 | loop fusion | flops 65536 | bytes 393216 | tf_op jit(solution)/shard_map/sub | solution.py:427
  (7 shorter events, 0.1 us)
Async XLA Ops:
  1.6 32.7 %copy-start.5 = (s32[8,2]{0,1:T(2,128)S(1)}, s32[8,2]{0,1:T(2,128)}, u32[]{:S(2)}) copy-start(s32[8,2]{0,1:T(2,128)} %param.9) | copy-start | bytes 196
  1.6 37.0 %copy-start.4 = (s32[8,256]{1,0:T(8,128)S(1)}, s32[8,256]{1,0:T(8,128)}, u32[]{:S(2)}) copy-start(s32[8,256]{1,0:T(8,128)} %order_ref.3) | copy-start | bytes 24580
  4.0 39.5 %collective-permute-start.3 = (f32[4,2,2,64,256]{4,3,2,1,0:T(8,128)}, f32[4,2,2,64,256]{4,3,2,1,0:T(8,128)}, u32[]{:S(2)}, u32[]{:S(2)}) collective-permute-start(f32[4,2,2,64,256]{4,3,2,1,0:T(8,128)} %dynamic-slice_multiply_fusion), channel_id=1, source_target_pairs={{4,0},{5,1},{510,2},{511,3},{8,4},{9,5},{2,6},{3,7},{12,8},{13,9},... | collective-permute-start | bytes 3145736 | tf_op jit(solution)/shard_map/ppermute | solution.py:361
  17.3 26.2 %copy-start = (f32[8,2,2,64,256]{4,3,2,1,0:T(8,128)S(1)}, f32[8,2,2,64,256]{4,3,2,1,0:T(8,128)}, u32[]{:S(2)}) copy-start(f32[8,2,2,64,256]{4,3,2,1,0:T(8,128)} %near_ref.3) | copy-start | bytes 6291460
  19.7 18.9 %all-to-all-start = ((f32[16,64,256]{2,1,0:T(8,128)}), f32[16,64,256]{2,1,0:T(8,128)S(1)}, u32[]{:S(2)}, u32[]{:S(2)}) async-start(f32[16,64,256]{2,1,0:T(8,128)} %get-tuple-element.24), calls=%async_computation | async-start | bytes 2097152 | tf_op jit(solution)/shard_map/all_to_all | solution.py:312
  23.8 25.3 %collective-permute-start = (f32[4,64,256]{2,1,0:T(8,128)}, f32[4,64,256]{2,1,0:T(8,128)S(1)}, u32[]{:S(2)}, u32[]{:S(2)}) collective-permute-start(f32[4,64,256]{2,1,0:T(8,128)} %get-tuple-element.21), channel_id=1, source_target_pairs={{0,1},{1,2},{2,3},{3,0},{4,5},{5,6},{6,7},{7,4},{8,9},{9,10},{10,1... | collective-permute-start | bytes 786440 | tf_op jit(solution)/shard_map/ppermute | solution.py:369
  27.1 22.0 %collective-permute-start.1 = (f32[4,64,256]{2,1,0:T(8,128)}, f32[4,64,256]{2,1,0:T(8,128)}, u32[]{:S(2)}, u32[]{:S(2)}) collective-permute-start(f32[4,64,256]{2,1,0:T(8,128)} %get-tuple-element.22), channel_id=1, source_target_pairs={{0,2},{1,3},{2,0},{3,1},{4,6},{5,7},{6,4},{7,5},{8,10},{9,11},{10,... | collective-permute-start | bytes 786440 | tf_op jit(solution)/shard_map/ppermute | solution.py:369
  29.7 19.4 %collective-permute-start.2 = (f32[4,64,256]{2,1,0:T(8,128)}, f32[4,64,256]{2,1,0:T(8,128)}, u32[]{:S(2)}, u32[]{:S(2)}) collective-permute-start(f32[4,64,256]{2,1,0:T(8,128)} %get-tuple-element.23), channel_id=1, source_target_pairs={{0,3},{1,0},{2,1},{3,2},{4,7},{5,4},{6,5},{7,6},{8,11},{9,8},{10,9... | collective-permute-start | bytes 786440 | tf_op jit(solution)/shard_map/ppermute | solution.py:369
  38.6 1.0 %copy-start.1 = (f32[8,64,192]{2,1,0:T(8,128)S(1)}, f32[8,64,192]{2,1,0:T(8,128)}, u32[]{:S(2)}) copy-start(f32[8,64,192]{2,1,0:T(8,128)} %interp_ref.3) | copy-start | bytes 1179652
  43.5 5.6 %copy-start.2 = (f32[8,64,192]{2,1,0:T(8,128)S(1)}, f32[8,64,192]{2,1,0:T(8,128)}, u32[]{:S(2)}) copy-start(f32[8,64,192]{2,1,0:T(8,128)} %interp_ref.3) | copy-start | bytes 1179652
  43.5 5.6 %copy-start.3 = (f32[8,64,256]{2,1,0:T(8,128)S(1)}, f32[8,64,256]{2,1,0:T(8,128)}, u32[]{:S(2)}) copy-start(f32[8,64,256]{2,1,0:T(8,128)} %block_ref.3) | copy-start | bytes 1572868
  47.1 9.6 %collective-permute-start.4 = (f32[4,64,128]{2,1,0:T(8,128)S(1)}, f32[4,64,128]{2,1,0:T(8,128)S(1)}, u32[]{:S(2)}, u32[]{:S(2)}) collective-permute-start(f32[4,64,128]{2,1,0:T(8,128)S(1)} %get-tuple-element.36), channel_id=1, source_target_pairs={{508,0},{509,1},{6,2},{7,3},{0,4},{1,5},{10,6},{11,7},{4,8},{5,9},... | collective-permute-start | bytes 393224 | tf_op jit(solution)/shard_map/ppermute | solution.py:404
